TPU v7x, 32 devices: a whole 2x2x4 slice. The times are simulated.
32 devices in a mesh: grp: 8 (over z, y), blk: 4 (over x, core).
Axes of the slice: x: 2, y: 2, z: 4, core: 2. Of those that a mesh axis runs over, the one named last changes fastest.
Arguments:
- query: bfloat16 [4096, 512], P(('grp', 'blk')), may hold values from -6 to 6
- key: bfloat16 [4096, 512], P(('grp', 'blk')), may hold values from -6 to 6
- value: bfloat16 [4096, 512], P(('grp', 'blk')), may hold values from -6 to 6
- gate_u: bfloat16 [4096, 512], P(('grp', 'blk')), may hold values from -6 to 6
- out_grad: bfloat16 [4096, 1024], P(('grp', 'blk')), may hold values from -6 to 6
- lengths: int32 [8], P('grp'), may hold values from 32 to 512
- norm_gain: float32 [512], replicated, may hold values from 0.1 to 1.9
- out_weight: bfloat16 [512, 1024], replicated, may hold values from -0.25 to 0.25
Outputs:
- layer_out: bfloat16 [4096, 1024], P(('grp', 'blk'))
- grad_query: bfloat16 [4096, 512], P(('grp', 'blk'))
- grad_key: bfloat16 [4096, 512], P(('grp', 'blk'))
- grad_value: bfloat16 [4096, 512], P(('grp', 'blk'))
- grad_gate: bfloat16 [4096, 512], P(('grp', 'blk'))
- grad_weight: float32 [512, 1024], P(None, 'blk')
Inputs may be any that keep to these rules, and one draw needn't show every extreme that they name: `lengths`: events of a user at or past its length are padding.
All inputs are finite; a program needn't handle non-finite values.
Results may differ from a plain program's by a relative error of at most 0.009.
Values may be sent and summed in bfloat16 or wider, within the bound.
No kernel may reach another device: no remote copies, remote signals or barrier semaphores. Data moves between devices by JAX's collectives and lax.ppermute only.
A program may use at most 64 MiB of HBM per device.

v0:
```python
import math
import jax
import jax.numpy as jnp
from jax import lax
from jax.sharding import PartitionSpec as P

HEADS = 8
HEAD = 64
EPS = 1e-05


def causal_mask(query_pos, key_pos, length):
    return (
        (key_pos[None, :] <= query_pos[:, None])
        & (query_pos[:, None] < length)
        & (key_pos[None, :] < length)
    )


def over_blocks(total_rows, step_fn, initial):
    size = math.gcd(total_rows, 512)

    def advance(index, carry):
        return step_fn(carry, index * size, size)

    return lax.fori_loop(0, total_rows // size, advance, initial)


def shards(query, key, value, gate_u, out_grad, lengths, norm_gain, out_weight):
    rows = query.shape[0]
    scale = HEAD ** (-0.5)
    length = lengths[0]
    lanes = lax.axis_size("blk")
    position = lax.axis_index("blk")
    first_row = position * rows
    row_pos = first_row + jnp.arange(rows, dtype=jnp.int32)
    total_len = rows * lanes
    query_heads = query.reshape(rows, HEADS, HEAD)
    key_heads = key.reshape(rows, HEADS, HEAD)
    value_heads = value.reshape(rows, HEADS, HEAD)
    zeros = jnp.zeros((rows, HEADS, HEAD), jnp.float32)
    keys_all, values_all = (
        lax.all_gather(key, "blk", axis=0, tiled=True),
        lax.all_gather(value, "blk", axis=0, tiled=True),
    )

    def forward_step(carry, begin, size):
        key_block = lax.dynamic_slice_in_dim(keys_all, begin, size, 0).reshape(size, HEADS, HEAD)
        value_block = lax.dynamic_slice_in_dim(values_all, begin, size, 0).reshape(
            size, HEADS, HEAD
        )
        scores = (
            jnp.einsum("rhd,nhd->hrn", query_heads, key_block, preferred_element_type=jnp.float32)
            * scale
        )
        mask = causal_mask(row_pos, begin + jnp.arange(size, dtype=jnp.int32), length)
        weights = (jax.nn.silu(scores) * mask[None]).astype(jnp.bfloat16)
        return carry + jnp.einsum(
            "hrn,nhd->rhd", weights, value_block, preferred_element_type=jnp.float32
        )

    attended = over_blocks(total_len, forward_step, zeros).reshape(rows, HEADS * HEAD)
    centre = attended - jnp.mean(attended, axis=1, keepdims=True)
    inv_std = lax.rsqrt(jnp.mean(centre * centre, axis=1, keepdims=True) + EPS)
    normed = centre * inv_std
    scaled = normed * norm_gain
    gates = gate_u.astype(jnp.float32)
    mixed = (scaled * gates).astype(jnp.bfloat16)
    layer_out = jnp.dot(mixed, out_weight, preferred_element_type=jnp.float32).astype(jnp.bfloat16)
    mixed_grad = lax.dot_general(
        out_grad, out_weight, (((1,), (1,)), ((), ())), preferred_element_type=jnp.float32
    )
    grad_gate = (mixed_grad * scaled).astype(jnp.bfloat16)
    normed_grad = mixed_grad * gates * norm_gain
    attended_grad = inv_std * (
        normed_grad
        - jnp.mean(normed_grad, axis=1, keepdims=True)
        - normed * jnp.mean(normed_grad * normed, axis=1, keepdims=True)
    )
    attended_grad = attended_grad.astype(jnp.bfloat16)
    grad_heads = attended_grad.reshape(rows, HEADS, HEAD)
    weight_term = lax.dot_general(
        mixed, out_grad, (((0,), (0,)), ((), ())), preferred_element_type=jnp.float32
    )

    def query_step(carry, begin, size):
        key_block = lax.dynamic_slice_in_dim(keys_all, begin, size, 0).reshape(size, HEADS, HEAD)
        value_block = lax.dynamic_slice_in_dim(values_all, begin, size, 0).reshape(
            size, HEADS, HEAD
        )
        scores = (
            jnp.einsum("rhd,nhd->hrn", query_heads, key_block, preferred_element_type=jnp.float32)
            * scale
        )
        mask = causal_mask(row_pos, begin + jnp.arange(size, dtype=jnp.int32), length)
        sigma = jax.nn.sigmoid(scores)
        prob_grad = jnp.einsum(
            "rhd,nhd->hrn", grad_heads, value_block, preferred_element_type=jnp.float32
        )
        score_grad = (prob_grad * sigma * (1.0 + scores * (1.0 - sigma)) * mask[None]).astype(
            jnp.bfloat16
        )
        return carry + jnp.einsum(
            "hrn,nhd->rhd", score_grad, key_block, preferred_element_type=jnp.float32
        )

    grad_query = (
        (over_blocks(total_len, query_step, zeros) * scale)
        .reshape(rows, HEADS * HEAD)
        .astype(jnp.bfloat16)
    )
    query_piece = lax.all_gather(query, "blk", axis=0, tiled=True)
    grad_piece = lax.all_gather(attended_grad, "blk", axis=0, tiled=True)
    count = query_piece.shape[0]

    def inner(acc, begin, size):
        key_acc, value_acc = acc
        query_block = lax.dynamic_slice_in_dim(query_piece, begin, size, 0).reshape(
            size, HEADS, HEAD
        )
        grad_block = lax.dynamic_slice_in_dim(grad_piece, begin, size, 0).reshape(size, HEADS, HEAD)
        scores = (
            jnp.einsum("nhd,rhd->hnr", query_block, key_heads, preferred_element_type=jnp.float32)
            * scale
        )
        mask = causal_mask(begin + jnp.arange(size, dtype=jnp.int32), row_pos, length)
        weights = (jax.nn.silu(scores) * mask[None]).astype(jnp.bfloat16)
        sigma = jax.nn.sigmoid(scores)
        prob_grad = jnp.einsum(
            "nhd,rhd->hnr", grad_block, value_heads, preferred_element_type=jnp.float32
        )
        score_grad = (prob_grad * sigma * (1.0 + scores * (1.0 - sigma)) * mask[None]).astype(
            jnp.bfloat16
        )
        key_acc = key_acc + jnp.einsum(
            "hnr,nhd->rhd", score_grad, query_block, preferred_element_type=jnp.float32
        )
        value_acc = value_acc + jnp.einsum(
            "hnr,nhd->rhd", weights, grad_block, preferred_element_type=jnp.float32
        )
        return (key_acc, value_acc)

    key_acc, value_acc = over_blocks(count, inner, (zeros, zeros))
    grad_key = (key_acc * scale).reshape(rows, HEADS * HEAD).astype(jnp.bfloat16)
    grad_value = value_acc.reshape(rows, HEADS * HEAD).astype(jnp.bfloat16)
    column_part = lax.psum_scatter(weight_term, "blk", scatter_dimension=1, tiled=True)
    grad_weight = lax.psum(column_part, "grp")
    return (layer_out, grad_query, grad_key, grad_value, grad_gate, grad_weight)


def solution(mesh):
    return jax.shard_map(
        shards,
        mesh=mesh,
        in_specs=(
            P(("grp", "blk"), None),
            P(("grp", "blk"), None),
            P(("grp", "blk"), None),
            P(("grp", "blk"), None),
            P(("grp", "blk"), None),
            P("grp"),
            P(),
            P(),
        ),
        out_specs=(
            P(("grp", "blk"), None),
            P(("grp", "blk"), None),
            P(("grp", "blk"), None),
            P(("grp", "blk"), None),
            P(("grp", "blk"), None),
            P(None, "blk"),
        ),
        check_vma=False,
    )
```

profile of v0, /device:TPU:0, one launch (start us, length us, event | category | flops | bytes accessed | tf_op | source)
XLA Modules:
  0.0 158.3 jit_solution(8994347896110078273)
XLA Ops:
  7.2 0.0 copy-start
  7.2 0.0 reduce-scatter.2.cloned.1.call-start
  7.2 9.0 %all_gather.13 = bf16[512,512]{1,0:T(8,128)(2,1)S(1)} all-gather(bf16[128,512]{1,0:T(8,128)(2,1)} %param.10), channel_id=1, replica_groups=mesh['grp'=8,'blk'=4] {'blk'}, dimensions={0}, use_global_device_ids=true | all-gather | bytes 655360 | tf_op jit(solution)/shard_map/all_gather | solution.py:44
  16.2 1.0 copy.26
  17.2 1.0 copy.24
  18.3 7.5 %all_gather.12 = bf16[512,512]{1,0:T(8,128)(2,1)S(1)} all-gather(bf16[128,512]{1,0:T(8,128)(2,1)} %param.9), channel_id=1, replica_groups=mesh['grp'=8,'blk'=4] {'blk'}, dimensions={0}, use_global_device_ids=true | all-gather | bytes 655360 | tf_op jit(solution)/shard_map/all_gather | solution.py:43
  25.7 1.0 copy.25
  27.5 1.5 fusion.33
  29.0 0.1 fusion.19
  29.1 0.0 copy-start.9
  29.1 0.0 copy-start.12
  29.1 2.0 %fusion.32 = (f32[128]{0:T(128)S(1)}, f32[8,128,64]{1,2,0:T(8,128)S(1)}) fusion(bf16[512,8,64]{0,2,1:T(8,128)(2,1)} %bitcast.51, f32[8,128,512]{2,1,0:T(8,128)S(1)} %fusion.33, f32[128,512]{1,0:T(8,128)S(1)} %fusion.19), kind=kOutput, calls=%fused_computation.56 | convolution fusion | flops 70844288 | bytes 3146240 | tf_op jit(solution)/shard_map/while/body/eval_jaxpr/hrn,nhd->rhd/dot_general | solution.py:58
  31.2 0.0 copy-done.13
  31.2 0.0 copy-done.10
  31.2 0.0 copy-start.4
  31.2 0.1 fusion.16
  31.3 0.5 add_rsqrt_fusion
  31.8 0.1 copy-done.4
  31.9 1.1 copy.27
  33.0 0.0 copy-start.3
  33.0 1.6 %fusion.23 = (f32[128]{0:T(128)S(1)}, f32[128]{0:T(128)S(1)}, f32[128,512]{1,0:T(8,128)S(1)}) fusion(f32[512]{0:T(512)S(1)} %copy-done.12, bf16[128,512]{1,0:T(8,128)(2,1)S(1)} %copy-done.9, f32[128]{0:T(128)} %add_rsqrt_fusion, f32[128,512]{1,0:T(8,128)S(1)} %copy.27, f32[128]{0:T(128)S(1)} %broadcast_multiply_fusion.2, bf16[128,1024]{1,0:T(8,128)(2,1)} %param.12, ...), kind=kOutput, calls=%fused_computation.40 | convolution fusion | flops 134741760 | bytes 1970176 | tf_op jit(solution)/shard_map/dot_general | solution.py:70
  34.6 1.8 %multiply_convert_fusion.6 = (bf16[128,512]{1,0:T(8,128)(2,1)}, bf16[128,512]{1,0:T(8,128)(2,1)S(1)}, bf16[128,512]{1,0:T(8,128)(2,1)S(1)}) fusion(f32[128,512]{1,0:T(8,128)S(1)} %get-tuple-element.96, f32[128,512]{1,0:T(8,128)S(1)} %copy.27, f32[512]{0:T(512)S(1)} %copy-done.12, f32[128]{0:T(128)} %add_rsqrt_fusion, f32[128]{0:T(128)S(1)} %broadcast_multiply_fusion.2, ...), kind=kLoop, calls=%fused_computation.28 | loop fusion | flops 983040 | bytes 1052672 | tf_op jit(solution)/shard_map/convert_element_type | solution.py:73
  36.4 0.6 copy-done.1
  37.0 1.8 %fusion.35 = f32[512,1024]{1,0:T(8,128)} fusion(bf16[128,512]{1,0:T(8,128)(2,1)S(1)} %get-tuple-element.93, bf16[128,1024]{1,0:T(8,128)(2,1)S(1)} %copy-done.3), kind=kOutput, calls=%fused_computation.59 | convolution fusion | flops 134217728 | bytes 2490368 | tf_op jit(solution)/shard_map/dot_general | solution.py:82
  38.9 0.0 reduce-scatter.2.cloned.1.call-update
  38.9 0.0 all-reduce.2.cloned.1.call-start
  38.9 0.8 copy.32
  39.7 0.7 copy.30
  40.4 0.1 copy.28
  40.6 0.0 copy-start.7
  40.6 3.3 %fusion.5 = bf16[8,128,64]{1,2,0:T(8,128)(2,1)} fusion(bf16[512,8,64]{0,2,1:T(8,128)(2,1)} %bitcast.47, f32[8,128,512]{2,1,0:T(8,128)S(1)} %fusion.33, bf16[128,8,64]{0,2,1:T(8,128)(2,1)S(1)} %bitcast.59, bf16[512,8,64]{0,2,1:T(8,128)(2,1)} %bitcast.52, f32[128,512]{1,0:T(8,128)} %copy-done.10), kind=kOutput, calls=%fused_computation.12 | convolution fusion | flops 140115968 | bytes 3670016 | tf_op jit(solution)/shard_map/while/body/eval_jaxpr/hrn,nhd->rhd/dot_general | solution.py:103
  43.9 1.7 %copy.33 = bf16[128,512]{1,0:T(8,128)(2,1)} copy(bf16[128,512]{0,1:T(8,128)(2,1)} %bitcast.58) | data formatting | bytes 262144
  45.6 7.3 %all_gather.15 = bf16[512,512]{1,0:T(8,128)(2,1)S(1)} all-gather(bf16[128,512]{1,0:T(8,128)(2,1)S(1)} %copy-done.7), channel_id=1, replica_groups=mesh['grp'=8,'blk'=4] {'blk'}, dimensions={0}, use_global_device_ids=true | all-gather | bytes 655360 | tf_op jit(solution)/shard_map/all_gather | solution.py:112
  52.8 1.0 copy.31
  53.8 9.5 %all_gather.14 = bf16[512,512]{1,0:T(8,128)(2,1)S(1)} all-gather(bf16[128,512]{1,0:T(8,128)(2,1)S(1)} %get-tuple-element.92), channel_id=1, replica_groups=mesh['grp'=8,'blk'=4] {'blk'}, dimensions={0}, use_global_device_ids=true | all-gather | bytes 655360 | tf_op jit(solution)/shard_map/all_gather | solution.py:113
  63.3 1.0 copy.29
  64.3 0.1 fusion.22
  64.5 0.0 copy-start.11
  64.5 1.6 %fusion.34 = f32[8,512,128]{2,1,0:T(8,128)S(1)} fusion(bf16[512,8,64]{0,2,1:T(8,128)(2,1)} %bitcast.48, bf16[128,8,64]{0,2,1:T(8,128)(2,1)S(1)} %bitcast.55), kind=kOutput, calls=%fused_computation.58 | convolution fusion | flops 67108864 | bytes 2752512 | tf_op jit(solution)/shard_map/while/body/eval_jaxpr/nhd,rhd->hnr/dot_general | solution.py:123
  66.2 2.6 %fusion.4 = bf16[8,128,64]{1,2,0:T(8,128)(2,1)S(1)} fusion(bf16[512,8,64]{0,2,1:T(8,128)(2,1)} %bitcast.49, f32[8,512,128]{2,1,0:T(8,128)S(1)} %fusion.34, bf16[512,8,64]{0,2,1:T(8,128)(2,1)} %bitcast.53, bf16[128,8,64]{0,2,1:T(8,128)(2,1)} %bitcast.57, f32[512,128]{1,0:T(8,128)S(1)} %fusion.22), kind=kOutput, calls=%fused_computation.11 | convolution fusion | flops 140115968 | bytes 3670016 | tf_op jit(solution)/shard_map/while/body/eval_jaxpr/hnr,nhd->rhd/dot_general | solution.py:135
  68.8 0.8 copy.34
  69.5 3.2 %reduce-scatter.2.cloned.1.call-done = f32[512,256]{1,0:T(8,128)} async-done(((f32[512,1024]{1,0:T(8,128)}), f32[512,256]{1,0:T(8,128)}) %reduce-scatter.2.cloned.1.call-update) | async-done | bytes 524304 | tf_op jit(solution)/shard_map/reduce_scatter | solution.py:146
  72.7 0.0 all-reduce.2.cloned.1.call-update
  72.7 2.0 %convolution_convert_fusion.1 = bf16[8,64,128]{2,1,0:T(8,128)(2,1)S(1)} fusion(bf16[512,8,64]{0,2,1:T(8,128)(2,1)} %bitcast.54, f32[8,512,128]{2,1,0:T(8,128)S(1)} %fusion.34, f32[512,128]{1,0:T(8,128)} %copy-done.11), kind=kOutput, calls=%fused_computation.13 | convolution fusion | flops 70844416 | bytes 3014656 | tf_op jit(solution)/shard_map/while/body/eval_jaxpr/hnr,nhd->rhd/dot_general | solution.py:138
  74.7 0.8 copy.35
  75.5 1.0 convolution_convert_fusion
  76.5 73.1 %all-reduce.2.cloned.1.call-done = f32[512,256]{1,0:T(8,128)} async-done(((f32[512,256]{1,0:T(8,128)}), f32[512,256]{1,0:T(8,128)}) %all-reduce.2.cloned.1.call-update) | async-done | bytes 524304 | tf_op jit(solution)/shard_map/psum | solution.py:147
  149.6 1.9 %copy.38 = f32[512,256]{1,0:T(8,128)} copy(f32[512,256]{1,0:T(8,128)} %all-reduce.2.cloned.1.call-done) | data formatting | bytes 1048576
  (24 shorter events, 0.1 us)
Async XLA Ops:
  7.2 25.8 %copy-start = (bf16[512,1024]{1,0:T(8,128)(2,1)S(1)}, bf16[512,1024]{1,0:T(8,128)(2,1)}, u32[]{:S(2)}) copy-start(bf16[512,1024]{1,0:T(8,128)(2,1)} %param.15) | copy-start | bytes 3145732
  7.2 65.5 %reduce-scatter.2.cloned.1.call-start = ((), (), s32[]{:S(2)}) async-start(), calls=%async_computation.1 | async-start | bytes 2621440 | tf_op jit(solution)/shard_map/reduce_scatter | solution.py:146
  27.4 3.7 %copy-start.13 = (pred[512]{0:T(512)(128)(4,1)}, pred[512]{0:T(512)(128)(4,1)S(1)}, u32[]{:S(2)}) copy-start(pred[512]{0:T(512)(128)(4,1)S(1)} %iota_compare_fusion.2) | copy-start | bytes 1540
  29.1 2.1 %copy-start.10 = (f32[128,512]{1,0:T(8,128)}, f32[128,512]{1,0:T(8,128)S(1)}, u32[]{:S(2)}) copy-start(f32[128,512]{1,0:T(8,128)S(1)} %fusion.19) | copy-start | bytes 786436
  29.1 3.9 %copy-start.9 = (bf16[128,512]{1,0:T(8,128)(2,1)S(1)}, bf16[128,512]{1,0:T(8,128)(2,1)}, u32[]{:S(2)}) copy-start(bf16[128,512]{1,0:T(8,128)(2,1)} %param.11) | copy-start | bytes 393220
  29.1 3.9 %copy-start.12 = (f32[512]{0:T(512)S(1)}, f32[512]{0:T(512)}, u32[]{:S(2)}) copy-start(f32[512]{0:T(512)} %param.14) | copy-start | bytes 6148
  31.2 0.7 copy-start.4
  33.0 4.0 %copy-start.3 = (bf16[128,1024]{1,0:T(8,128)(2,1)S(1)}, bf16[128,1024]{1,0:T(8,128)(2,1)}, u32[]{:S(2)}) copy-start(bf16[128,1024]{1,0:T(8,128)(2,1)} %param.12) | copy-start | bytes 786436
  36.4 0.6 copy-start.1
  37.0 1.9 %copy-start.5 = (bf16[128,512]{1,0:T(8,128)(2,1)S(1)}, bf16[128,512]{1,0:T(8,128)(2,1)}, u32[]{:S(2)}) copy-start(bf16[128,512]{1,0:T(8,128)(2,1)} %param.9) | copy-start | bytes 393220
  37.0 2.7 %copy-start.6 = (bf16[128,512]{1,0:T(8,128)(2,1)S(1)}, bf16[128,512]{1,0:T(8,128)(2,1)}, u32[]{:S(2)}) copy-start(bf16[128,512]{1,0:T(8,128)(2,1)} %param.10) | copy-start | bytes 393220
  38.9 110.8 %all-reduce.2.cloned.1.call-start = ((), (), s32[]{:S(2)}) async-start(), calls=%async_computation.2 | async-start | bytes 1048576 | tf_op jit(solution)/shard_map/psum | solution.py:147
  40.6 5.0 %copy-start.7 = (bf16[128,512]{1,0:T(8,128)(2,1)S(1)}, bf16[128,512]{1,0:T(8,128)(2,1)}, u32[]{:S(2)}) copy-start(bf16[128,512]{1,0:T(8,128)(2,1)} %param.8) | copy-start | bytes 393220
  43.9 20.5 %copy-start.14 = (pred[512]{0:T(512)(128)(4,1)S(1)}, pred[512]{0:T(512)(128)(4,1)}, u32[]{:S(2)}) copy-start(pred[512]{0:T(512)(128)(4,1)} %copy-done.13) | copy-start | bytes 1540
  43.9 20.6 %copy-start.8 = (bf16[128,512]{0,1:T(8,128)(2,1)S(1)}, bf16[128,512]{0,1:T(8,128)(2,1)}, u32[]{:S(2)}) copy-start(bf16[128,512]{0,1:T(8,128)(2,1)} %copy.32) | copy-start | bytes 393220
  64.5 4.3 %copy-start.11 = (f32[512,128]{1,0:T(8,128)}, f32[512,128]{1,0:T(8,128)S(1)}, u32[]{:S(2)}) copy-start(f32[512,128]{1,0:T(8,128)S(1)} %fusion.22) | copy-start | bytes 786436
  72.7 2.8 %copy-start.2 = (bf16[128,512]{1,0:T(8,128)(2,1)S(1)}, bf16[128,512]{1,0:T(8,128)(2,1)}, u32[]{:S(2)}) copy-start(bf16[128,512]{1,0:T(8,128)(2,1)} %copy-done.1) | copy-start | bytes 393220
Sparse Core Ops, SparseCore 0:
  39.0 33.6 reduce-scatter.1
  76.1 73.4 all-reduce.1
where the time goes:
time: 159 us; the launch traced here: 158 us
  waiting for transfers between devices  76.3 us (48%)
  blocking collectives  33.2 us (21%)
  matrix products  17.5 us (11%)
  between operations  14.9 us (9%)
  local copies, waits for them, and re-layouts  13.7 us (9%)
  other arithmetic  2.64 us (2%)
    psum x1, waiting for transfers between devices, shards(): grad_weight = lax.psum(column_part, 'grp')  73.1 us
    all_gather x1, blocking collectives, shards(): grad_piece = lax.all_gather(attended_grad, 'blk', axis=0, tiled=True)  9.49 us
    all_gather x1, blocking collectives, shards(): lax.all_gather(value, 'blk', axis=0, tiled=True)  8.99 us
    unnamed x37, local copies, waits for them, and re-layouts  8.42 us
    all_gather x1, blocking collectives, shards(): lax.all_gather(key, 'blk', axis=0, tiled=True)  7.49 us
    all_gather x1, blocking collectives, shards(): query_piece = lax.all_gather(query, 'blk', axis=0, tiled=True)  7.27 us
    dot_general x1, matrix products, query_step(): jnp.einsum('hrn,nhd->rhd', score_grad, key_block, preferred_element_type=...  3.29 us
  transfers between devices with their start and end apart: 2, of which 2 were waited for; matrix products, arithmetic and copies ran while one was open for 11% of the time, Pallas kernels for 0%

commit v1 on v0

--- a/solution.py
+++ b/solution.py
@@ -109,8 +109,11 @@
         .reshape(rows, HEADS * HEAD)
         .astype(jnp.bfloat16)
     )
-    query_piece = lax.all_gather(query, "blk", axis=0, tiled=True)
-    grad_piece = lax.all_gather(attended_grad, "blk", axis=0, tiled=True)
+    query_piece, grad_piece = jnp.split(
+        lax.all_gather(jnp.concatenate([query, attended_grad], axis=1), "blk", axis=0, tiled=True),
+        [query.shape[1]],
+        axis=1,
+    )
     count = query_piece.shape[0]
 
     def inner(acc, begin, size):

time: 159 us -> 175 us (1.10)
  waiting for transfers between devices: 76.3 us -> 107 us
  blocking collectives: 33.2 us -> 16.5 us
    reduce_scatter x1, waiting for transfers between devices: 3.17 us -> 28.9 us  [shards(): lax.psum_scatter(weight_term, 'blk', scatter_dimension=1, tiled=True)]
    all_gather x2 -> x0, blocking collectives: 16.8 us -> none  [the longest x1 9.49 us: shards(): grad_piece = lax.all_gather(attended_grad, 'blk', axis=0, tiled=True)]
    all_gather x0 -> x1, waiting for transfers between devices: none -> 7.79 us  [shards(): lax.all_gather(jnp.concatenate([query, attended_grad], axis=1), 'blk', ax...]
    split x0 -> x3, local copies, waits for them, and re-layouts: none -> 3.28 us  [shards(): jnp.split(lax.all_gather(jnp.concatenate([query, attended_grad], axis=1),...]
    psum x1, waiting for transfers between devices: 73.1 us -> 70.1 us  [shards(): grad_weight = lax.psum(column_part, 'grp')]
    all_gather x2 -> x0, local copies, waits for them, and re-layouts: 2.02 us -> none  [the longest x1 1.02 us: shards(): grad_piece = lax.all_gather(attended_grad, 'blk', axis=0, tiled=True)]
    unnamed x37 -> x29, local copies, waits for them, and re-layouts: 8.42 us -> 6.85 us
  transfers between devices with their start and end apart: 2 -> 3, of which waited for: 2 -> 3; matrix products, arithmetic and copies ran while one was open for 11% -> 12% of each run, Pallas kernels for 0% -> 0%
where the time goes in v1:
time: 175 us; the launch traced here: 174 us
  waiting for transfers between devices  107 us (61%)
  matrix products  17.6 us (10%)
  blocking collectives  16.5 us (9%)
  between operations  14.6 us (8%)
  local copies, waits for them, and re-layouts  14 us (8%)
  other arithmetic  4.32 us (2%)
    psum x1, waiting for transfers between devices, shards(): grad_weight = lax.psum(column_part, 'grp')  70.1 us
    reduce_scatter x1, waiting for transfers between devices, shards(): lax.psum_scatter(weight_term, 'blk', scatter_dimension=1, tiled=True)  28.9 us
    all_gather x1, blocking collectives, shards(): lax.all_gather(value, 'blk', axis=0, tiled=True)  8.99 us
    all_gather x1, waiting for transfers between devices, shards(): lax.all_gather(jnp.concatenate([query, attended_grad], axis=1), 'blk', ax...  7.79 us
    all_gather x1, blocking collectives, shards(): lax.all_gather(key, 'blk', axis=0, tiled=True)  7.49 us
    unnamed x29, local copies, waits for them, and re-layouts  6.85 us
  transfers between devices with their start and end apart: 3, of which 3 were waited for; matrix products, arithmetic and copies ran while one was open for 12% of the time, Pallas kernels for 0%

profile of v1, /device:TPU:0, one launch (start us, length us, event | category | flops | bytes accessed | tf_op | source)
XLA Modules:
  0.0 173.9 jit_solution(12305118625459041422)
XLA Ops:
  7.2 0.0 copy-start
  7.2 0.0 all-gather.2.cloned.1.call-start
  7.2 9.0 %all_gather.10 = bf16[512,512]{1,0:T(8,128)(2,1)S(1)} all-gather(bf16[128,512]{1,0:T(8,128)(2,1)} %param.10), channel_id=1, replica_groups=mesh['grp'=8,'blk'=4] {'blk'}, dimensions={0}, use_global_device_ids=true | all-gather | bytes 655360 | tf_op jit(solution)/shard_map/all_gather | solution.py:44
  16.2 1.0 copy.27
  17.2 1.0 copy.25
  18.3 7.5 %all_gather.9 = bf16[512,512]{1,0:T(8,128)(2,1)S(1)} all-gather(bf16[128,512]{1,0:T(8,128)(2,1)} %param.9), channel_id=1, replica_groups=mesh['grp'=8,'blk'=4] {'blk'}, dimensions={0}, use_global_device_ids=true | all-gather | bytes 655360 | tf_op jit(solution)/shard_map/all_gather | solution.py:43
  25.7 1.0 copy.26
  27.4 1.5 fusion.34
  29.0 0.1 fusion.19
  29.1 0.0 copy-start.7
  29.1 0.0 copy-start.6
  29.1 0.0 copy-start.8
  29.1 2.0 %fusion.33 = (f32[128]{0:T(128)S(1)}, f32[8,128,64]{1,2,0:T(8,128)S(1)}) fusion(bf16[512,8,64]{0,2,1:T(8,128)(2,1)} %bitcast.51, f32[8,128,512]{2,1,0:T(8,128)S(1)} %fusion.34, f32[128,512]{1,0:T(8,128)S(1)} %fusion.19), kind=kOutput, calls=%fused_computation.58 | convolution fusion | flops 70844288 | bytes 3146240 | tf_op jit(solution)/shard_map/while/body/eval_jaxpr/hrn,nhd->rhd/dot_general | solution.py:58
  31.2 0.0 copy-start.2
  31.2 0.1 fusion.16
  31.3 0.5 add_rsqrt_fusion
  31.8 0.1 copy-done.2
  31.9 1.1 copy.28
  33.0 1.5 fusion.23
  34.5 1.8 %multiply_convert_fusion.6 = (bf16[128,512]{1,0:T(8,128)(2,1)}, bf16[128,512]{1,0:T(8,128)(2,1)S(1)}, bf16[128,512]{1,0:T(8,128)(2,1)}) fusion(f32[128,512]{1,0:T(8,128)S(1)} %get-tuple-element.108, f32[128,512]{1,0:T(8,128)S(1)} %copy.28, f32[512]{0:T(512)S(1)} %copy-done.8, f32[128]{0:T(128)} %add_rsqrt_fusion, f32[128]{0:T(128)S(1)} %broadcast_multiply_fusion.2, ...), kind=kLoop, calls=%fused_computation.29 | loop fusion | flops 983040 | bytes 1052672 | tf_op jit(solution)/shard_map/convert_element_type | solution.py:73
  36.3 1.6 pad_maximum_fusion
  38.0 0.0 all-gather.2.cloned.1.call-update
  38.0 0.0 reduce-scatter.2.cloned.1.call-start
  38.1 0.0 copy-start.3
  38.1 0.0 copy-start.4
  38.1 2.9 %fusion.36 = f32[512,1024]{1,0:T(8,128)} fusion(bf16[128,512]{1,0:T(8,128)(2,1)} %get-tuple-element.95, bf16[128,1024]{1,0:T(8,128)(2,1)} %param.12), kind=kOutput, calls=%fused_computation.61 | convolution fusion | flops 134217728 | bytes 2490368 | tf_op jit(solution)/shard_map/dot_general | solution.py:82
  40.9 0.0 reduce-scatter.2.cloned.1.call-update
  41.0 0.0 all-reduce.2.cloned.1.call-start
  41.0 0.8 copy.29
  41.8 0.8 copy.33
  42.5 0.8 copy.32
  43.3 2.7 %fusion.5 = bf16[8,128,64]{1,2,0:T(8,128)(2,1)S(1)} fusion(bf16[512,8,64]{0,2,1:T(8,128)(2,1)} %bitcast.47, f32[8,128,512]{2,1,0:T(8,128)S(1)} %fusion.34, bf16[128,8,64]{0,2,1:T(8,128)(2,1)} %bitcast.58, bf16[512,8,64]{0,2,1:T(8,128)(2,1)} %bitcast.52, f32[128,512]{1,0:T(8,128)} %copy-done.7), kind=kOutput, calls=%fused_computation.12 | convolution fusion | flops 140115968 | bytes 3670016 | tf_op jit(solution)/shard_map/while/body/eval_jaxpr/hrn,nhd->rhd/dot_general | solution.py:103
  46.0 0.8 copy.34
  46.7 0.1 fusion.22
  46.9 1.0 convolution_convert_fusion
  47.9 7.8 %all-gather.2.cloned.1.call-done = bf16[512,1024]{1,0:T(8,128)(2,1)} async-done(((bf16[128,1024]{1,0:T(8,128)(2,1)}), bf16[512,1024]{1,0:T(8,128)(2,1)}) %all-gather.2.cloned.1.call-update) | async-done | bytes 1048592 | tf_op jit(solution)/shard_map/all_gather | solution.py:113
  55.7 1.3 fusion.32
  57.0 1.0 copy.30
  58.0 1.0 copy.31
  59.0 1.5 fusion.35
  60.5 28.9 %reduce-scatter.2.cloned.1.call-done = f32[512,256]{1,0:T(8,128)} async-done(((f32[512,1024]{1,0:T(8,128)}), f32[512,256]{1,0:T(8,128)}) %reduce-scatter.2.cloned.1.call-update) | async-done | bytes 524304 | tf_op jit(solution)/shard_map/reduce_scatter | solution.py:149
  89.4 0.0 all-reduce.2.cloned.1.call-update
  89.5 2.6 %fusion.4 = bf16[8,64,128]{2,1,0:T(8,128)(2,1)S(1)} fusion(bf16[512,8,64]{0,2,1:T(8,128)(2,1)} %bitcast.49, f32[8,512,128]{2,1,0:T(8,128)S(1)} %fusion.35, bf16[512,8,64]{0,2,1:T(8,128)(2,1)} %bitcast.53, bf16[128,8,64]{0,2,1:T(8,128)(2,1)} %bitcast.57, f32[512,128]{1,0:T(8,128)S(1)} %fusion.22), kind=kOutput, calls=%fused_computation.11 | convolution fusion | flops 140115968 | bytes 3670016 | tf_op jit(solution)/shard_map/while/body/eval_jaxpr/hnr,nhd->rhd/dot_general | solution.py:138
  92.0 0.8 copy.35
  92.8 1.9 %convolution_convert_fusion.1 = bf16[8,64,128]{2,1,0:T(8,128)(2,1)S(1)} fusion(bf16[512,8,64]{0,2,1:T(8,128)(2,1)} %bitcast.54, f32[8,512,128]{2,1,0:T(8,128)S(1)} %fusion.35, f32[512,128]{1,0:T(8,128)S(1)} %fusion.22), kind=kOutput, calls=%fused_computation.13 | convolution fusion | flops 70844416 | bytes 3014656 | tf_op jit(solution)/shard_map/while/body/eval_jaxpr/hnr,nhd->rhd/dot_general | solution.py:141
  94.7 0.8 copy.36
  95.5 70.1 %all-reduce.2.cloned.1.call-done = f32[512,256]{1,0:T(8,128)} async-done(((f32[512,256]{1,0:T(8,128)}), f32[512,256]{1,0:T(8,128)}) %all-reduce.2.cloned.1.call-update) | async-done | bytes 524304 | tf_op jit(solution)/shard_map/psum | solution.py:150
  165.5 1.9 %copy.39 = f32[512,256]{1,0:T(8,128)} copy(f32[512,256]{1,0:T(8,128)} %all-reduce.2.cloned.1.call-done) | data formatting | bytes 1048576
  (19 shorter events, 0.1 us)
Async XLA Ops:
  7.2 25.8 %copy-start = (bf16[512,1024]{1,0:T(8,128)(2,1)S(1)}, bf16[512,1024]{1,0:T(8,128)(2,1)}, u32[]{:S(2)}) copy-start(bf16[512,1024]{1,0:T(8,128)(2,1)} %param.15) | copy-start | bytes 3145732
  7.2 48.5 %all-gather.2.cloned.1.call-start = ((), (), s32[]{:S(2)}) async-start(), calls=%async_computation.1 | async-start | bytes 1310720 | tf_op jit(solution)/shard_map/all_gather | solution.py:113
  27.4 3.7 %copy-start.9 = (pred[512]{0:T(512)(128)(4,1)}, pred[512]{0:T(512)(128)(4,1)S(1)}, u32[]{:S(2)}) copy-start(pred[512]{0:T(512)(128)(4,1)S(1)} %iota_compare_fusion.2) | copy-start | bytes 1540
  29.1 2.1 %copy-start.7 = (f32[128,512]{1,0:T(8,128)}, f32[128,512]{1,0:T(8,128)S(1)}, u32[]{:S(2)}) copy-start(f32[128,512]{1,0:T(8,128)S(1)} %fusion.19) | copy-start | bytes 786436
  29.1 3.9 %copy-start.6 = (bf16[128,512]{1,0:T(8,128)(2,1)S(1)}, bf16[128,512]{1,0:T(8,128)(2,1)}, u32[]{:S(2)}) copy-start(bf16[128,512]{1,0:T(8,128)(2,1)} %param.11) | copy-start | bytes 393220
  29.1 3.9 %copy-start.8 = (f32[512]{0:T(512)S(1)}, f32[512]{0:T(512)}, u32[]{:S(2)}) copy-start(f32[512]{0:T(512)} %param.14) | copy-start | bytes 6148
  31.2 0.7 copy-start.2
  38.0 51.4 %reduce-scatter.2.cloned.1.call-start = ((), (), s32[]{:S(2)}) async-start(), calls=%async_computation.2 | async-start | bytes 2621440 | tf_op jit(solution)/shard_map/reduce_scatter | solution.py:149
  38.1 3.7 %copy-start.3 = (bf16[128,512]{1,0:T(8,128)(2,1)S(1)}, bf16[128,512]{1,0:T(8,128)(2,1)}, u32[]{:S(2)}) copy-start(bf16[128,512]{1,0:T(8,128)(2,1)} %param.9) | copy-start | bytes 393220
  38.1 4.5 %copy-start.4 = (bf16[128,512]{1,0:T(8,128)(2,1)S(1)}, bf16[128,512]{1,0:T(8,128)(2,1)}, u32[]{:S(2)}) copy-start(bf16[128,512]{1,0:T(8,128)(2,1)} %param.10) | copy-start | bytes 393220
  41.0 124.6 %all-reduce.2.cloned.1.call-start = ((), (), s32[]{:S(2)}) async-start(), calls=%async_computation.3 | async-start | bytes 1048576 | tf_op jit(solution)/shard_map/psum | solution.py:150
  43.3 3.5 %copy-start.10 = (pred[512]{0:T(512)(128)(4,1)S(1)}, pred[512]{0:T(512)(128)(4,1)}, u32[]{:S(2)}) copy-start(pred[512]{0:T(512)(128)(4,1)} %copy-done.9) | copy-start | bytes 1540
  43.3 3.6 %copy-start.1 = (bf16[128,512]{1,0:T(8,128)(2,1)S(1)}, bf16[128,512]{1,0:T(8,128)(2,1)}, u32[]{:S(2)}) copy-start(bf16[128,512]{1,0:T(8,128)(2,1)} %get-tuple-element.95) | copy-start | bytes 393220
  47.9 11.1 %copy-start.5 = (bf16[128,512]{0,1:T(8,128)(2,1)S(1)}, bf16[128,512]{0,1:T(8,128)(2,1)}, u32[]{:S(2)}) copy-start(bf16[128,512]{0,1:T(8,128)(2,1)} %copy.33) | copy-start | bytes 393220
Sparse Core Ops, SparseCore 0:
  38.1 17.5 all-gather.1
  58.2 31.1 reduce-scatter.1
  92.9 72.6 all-reduce.1
